TPU v7x, 32 devices: a whole 2x2x4 slice. The times are simulated.
32 devices in a mesh: sp: 4 (over x, core), tp: 8 (over z, y).
Axes of the slice: x: 2, y: 2, z: 4, core: 2. Of those that a mesh axis runs over, the one named last changes fastest.
Arguments:
- tokens: bfloat16 [8, 220, 4096], P(None, 'sp'), may hold values from -6 to 6
- modulation: float32 [6, 4096], replicated, may hold values from -2.5 to 2.5
- w_qkv: bfloat16 [4096, 3, 4096], P('sp', None, 'tp'), may hold values from -4 to 4
- w_out: bfloat16 [4096, 4096], P('tp', 'sp'), may hold values from -0.09375 to 0.09375
- w_up: bfloat16 [4096, 16384], P('sp', 'tp'), may hold values from -0.09375 to 0.09375
- w_down: bfloat16 [16384, 4096], P('tp', 'sp'), may hold values from -0.046875 to 0.046875
Outputs:
- block_out: bfloat16 [8, 220, 4096], P(None, 'sp', 'tp')
All inputs are finite; a program needn't handle non-finite values.
Results may differ from a plain program's by a relative error of at most 0.012.
Values may be sent and summed in bfloat16 or wider, within the bound.
No kernel may reach another device: no remote copies, remote signals or barrier semaphores. Data moves between devices by JAX's collectives and lax.ppermute only.
A program may use at most 128 MiB of HBM per device.

v0:
```python
import jax
import jax.numpy as jnp
from jax import lax
from jax.sharding import PartitionSpec as P

DH = 128
EPSILON = 1e-06


def normalize(tok_rows, shift_vec, scale_vec):
    values = tok_rows.astype(jnp.float32)
    center = jnp.mean(values, axis=-1, keepdims=True)
    spread = jnp.mean(jnp.square(values - center), axis=-1, keepdims=True)
    scaled = (values - center) * lax.rsqrt(spread + EPSILON)
    return (scaled * (1.0 + scale_vec) + shift_vec).astype(jnp.bfloat16)


def project_rows(operand, weight, einsum_form):
    return jnp.einsum(
        einsum_form,
        operand,
        lax.all_gather(weight, "sp", axis=0, tiled=True),
        preferred_element_type=jnp.float32,
    )


def project_cols(operand, weight, einsum_form, leading):
    portion = lax.all_gather(weight, "sp", axis=1, tiled=True)
    shaped = portion.reshape(leading + (portion.shape[1],))
    return jnp.einsum(einsum_form, operand, shaped, preferred_element_type=jnp.float32)


def attend_items(pieces):
    queries, key_rows, values = pieces
    factor = queries.shape[-1] ** (-0.5)

    def single(triple):
        query_one, key_one, value_one = triple
        scores = (
            lax.dot_general(
                query_one, key_one, (((1,), (1,)), ((), ())), preferred_element_type=jnp.float32
            )
            * factor
        )
        row_max = jnp.max(scores, axis=1, keepdims=True)
        raw_weights = jnp.exp(scores - row_max)
        att_weights = (raw_weights / jnp.sum(raw_weights, axis=1, keepdims=True)).astype(
            jnp.bfloat16
        )
        return jnp.dot(att_weights, value_one, preferred_element_type=jnp.float32).astype(
            jnp.bfloat16
        )

    result = lax.map(single, (queries[0], key_rows[0], values[0]))
    return result[None]


def attention_combine(base, partial_value, gate):
    summed = lax.psum(partial_value.astype(jnp.bfloat16), "tp").astype(jnp.float32)
    full = (base.astype(jnp.float32) + gate * summed).astype(jnp.bfloat16)
    return full


def mlp_combine(base, partial_value, gate):
    tp_count = lax.axis_size("tp")
    width = base.shape[2] // tp_count
    offset = lax.axis_index("tp") * width
    base_mine = lax.dynamic_slice_in_dim(base, offset, width, 2).astype(jnp.float32)
    gate_mine = lax.dynamic_slice_in_dim(gate, offset, width, 0)
    share = lax.psum_scatter(
        partial_value.astype(jnp.bfloat16), "tp", scatter_dimension=2, tiled=True
    ).astype(jnp.float32)
    return (base_mine + gate_mine * share).astype(jnp.bfloat16)


def shards(tokens, modulation, w_qkv, w_out, w_up, w_down):
    frames, patches, width = tokens.shape
    heads_local = w_qkv.shape[2] // DH
    sp_count = lax.axis_size("sp")
    items_dev = heads_local * frames // sp_count
    mod_a = normalize(tokens, modulation[0], modulation[1])
    weight_qkv = w_qkv.reshape(w_qkv.shape[0], 3, heads_local, DH)
    projected = project_rows(mod_a, weight_qkv, "fpd,dshe->shfpe").astype(jnp.bfloat16)
    projected = projected.reshape(3, sp_count, items_dev, patches, DH)
    attended = attend_items(
        (
            lax.all_to_all(projected[0], "sp", split_axis=0, concat_axis=2, tiled=True),
            lax.all_to_all(projected[1], "sp", split_axis=0, concat_axis=2, tiled=True),
            lax.all_to_all(projected[2], "sp", split_axis=0, concat_axis=2, tiled=True),
        )
    )
    returned = lax.all_to_all(attended, "sp", split_axis=2, concat_axis=0, tiled=True)
    returned = returned.reshape(heads_local, frames, patches, DH)
    partial_attn = project_cols(returned, w_out, "hfpd,hde->fpe", (heads_local, DH))
    middle = attention_combine(tokens, partial_attn, modulation[2])
    mod_b = normalize(middle, modulation[3], modulation[4])
    up_proj = project_rows(mod_b, w_up, "fpd,dc->fpc")
    hidden = jax.nn.gelu(up_proj, approximate=True).astype(jnp.bfloat16)
    partial_mlp = project_cols(hidden, w_down, "fpk,kc->fpc", (w_down.shape[0],))
    return mlp_combine(middle, partial_mlp, modulation[5])


def solution(mesh):
    placed = (
        P(None, "sp", None),
        P(),
        P("sp", None, "tp"),
        P("tp", "sp"),
        P("sp", "tp"),
        P("tp", "sp"),
    )
    return jax.shard_map(
        shards, mesh=mesh, in_specs=placed, out_specs=P(None, "sp", "tp"), check_vma=False
    )
```

profile of v0, /device:TPU:0, one launch (start us, length us, event | category | flops | bytes accessed | tf_op | source)
XLA Modules:
  0.0 655.9 jit_solution(7131236097919553995)
XLA Ops:
  6.5 3.2 copy.22
  9.7 2.8 copy.23
  12.6 0.7 all-gather.7.cloned.1.call-update
  13.4 5.8 convert_reduce_fusion
  19.2 3.9 fusion.23
  23.1 74.4 %all-gather.5.cloned.1.call-done = bf16[4096,3,4,128]{3,0,2,1:T(8,128)(2,1)} async-done(((bf16[1024,3,4,128]{3,0,2,1:T(8,128)(2,1)}), bf16[4096,3,4,128]{3,0,2,1:T(8,128)(2,1)}) %all-gather.5.cloned.1.call-update) | async-done | bytes 12582928 | tf_op jit(solution)/shard_map/all_gather | solution.py:22
  97.5 18.3 %fusion.69 = bf16[3,4,8,55,128]{4,3,1,0,2:T(8,128)(2,1)S(1)} fusion(bf16[4096,3,4,128]{3,0,2,1:T(8,128)(2,1)} %all-gather.5.cloned.1.call-done, f32[4096]{0:T(1024)S(1)} %bitcast.107, f32[4096]{0:T(1024)S(1)} %bitcast.108, f32[8,55]{1,0:T(8,128)S(1)} %add_rsqrt_fusion.1, f32[8,55]{1,0:T(8,128)S(1)} %broadcast_multiply_fusion.1, bf16[8,55,4096]{2,0,1:T(8,128)(2,1)} %param.8), kind=kOutput, calls=%fused_computation.64 | convolution fusion | flops 5547970560 | bytes 17575360 | tf_op jit(solution)/shard_map/fpd,dshe->shfpe/dot_general | solution.py:19
  115.9 0.9 copy.24
  116.9 3.5 all-to-all-start
  120.3 0.9 copy.25
  121.3 12.3 %all-to-all-done = bf16[4,8,55,128]{3,1,2,0:T(8,128)(2,1)S(1)} async-done(((bf16[4,8,55,128]{3,1,2,0:T(8,128)(2,1)}), bf16[4,8,55,128]{3,1,2,0:T(8,128)(2,1)S(1)}, u32[]{:S(2)}, u32[]{:S(2)}) %all-to-all-start) | async-done | bytes 450592 | tf_op jit(solution)/shard_map/all_to_all | solution.py:87
  133.6 3.5 all-to-all-start.1
  137.1 0.9 copy.26
  138.0 7.0 %all-to-all-done.1 = bf16[4,8,55,128]{3,1,2,0:T(8,128)(2,1)S(1)} async-done(((bf16[4,8,55,128]{3,1,2,0:T(8,128)(2,1)}), bf16[4,8,55,128]{3,1,2,0:T(8,128)(2,1)S(1)}, u32[]{:S(2)}, u32[]{:S(2)}) %all-to-all-start.1) | async-done | bytes 450592 | tf_op jit(solution)/shard_map/all_to_all | solution.py:88
  145.0 3.5 all-to-all-start.2
  148.7 7.8 %all-to-all-done.2 = bf16[4,8,55,128]{3,1,2,0:T(8,128)(2,1)S(1)} async-done(((bf16[4,8,55,128]{3,1,2,0:T(8,128)(2,1)}), bf16[4,8,55,128]{3,1,2,0:T(8,128)(2,1)S(1)}, u32[]{:S(2)}, u32[]{:S(2)}) %all-to-all-start.2) | async-done | bytes 450592 | tf_op jit(solution)/shard_map/all_to_all | solution.py:89
  156.6 4.6 while.10
  161.2 0.9 copy.52
  162.1 3.5 all-to-all-start.3
  165.6 7.9 %all-to-all-done.3 = bf16[1,8,220,128]{3,1,0,2:T(8,128)(2,1)S(1)} async-done(((bf16[1,8,220,128]{3,1,0,2:T(8,128)(2,1)}), bf16[1,8,220,128]{3,1,0,2:T(8,128)(2,1)S(1)}, u32[]{:S(2)}, u32[]{:S(2)}) %all-to-all-start.3) | async-done | bytes 450592 | tf_op jit(solution)/shard_map/all_to_all | solution.py:92
  173.6 5.7 bitcast_convert_fusion
  180.0 0.5 all-gather.9.cloned.1.call-update
  180.8 141.6 %all-reduce.2.cloned.1.call-done = bf16[8,55,4096]{2,1,0:T(8,128)(2,1)} async-done(((bf16[8,55,4096]{2,1,0:T(8,128)(2,1)}), bf16[8,55,4096]{2,1,0:T(8,128)(2,1)}) %all-reduce.2.cloned.1.call-update) | async-done | bytes 3604496 | tf_op jit(solution)/shard_map/psum | solution.py:59
  322.4 8.3 %convert_reduce_fusion.1 = (f32[8,55]{1,0:T(8,128)S(1)}, bf16[8,55,4096]{2,1,0:T(8,128)(2,1)S(1)}) fusion(bf16[8,55,4096]{2,1,0:T(8,128)(2,1)} %all-reduce.2.cloned.1.call-done, f32[4096]{0:T(1024)S(1)} %bitcast.104, bf16[8,55,4096]{2,0,1:T(8,128)(2,1)} %param.8), kind=kLoop, calls=%fused_computation.27 | loop fusion | flops 12615240 | bytes 10831584 | tf_op jit(solution)/shard_map/reduce_sum | solution.py:12
  330.7 2.0 copy-done.1
  332.7 1.1 fusion.27
  333.8 94.7 %all-gather.11.cloned.1.call-done = bf16[2048,4096]{1,0:T(8,128)(2,1)} async-done(((bf16[2048,1024]{1,0:T(8,128)(2,1)}), bf16[2048,4096]{1,0:T(8,128)(2,1)}) %all-gather.11.cloned.1.call-update) | async-done | bytes 16777232 | tf_op jit(solution)/shard_map/all_gather | solution.py:28
  428.5 107.3 %all-gather.9.cloned.1.call-done = bf16[4096,2048]{1,0:T(8,128)(2,1)} async-done(((bf16[1024,2048]{1,0:T(8,128)(2,1)}), bf16[4096,2048]{1,0:T(8,128)(2,1)}) %all-gather.9.cloned.1.call-update) | async-done | bytes 16777232 | tf_op jit(solution)/shard_map/all_gather | solution.py:22
  535.9 29.4 %fusion.32 = bf16[8,55,4096]{2,1,0:T(8,128)(2,1)} fusion(bf16[2048,4096]{1,0:T(8,128)(2,1)} %all-gather.11.cloned.1.call-done, bf16[4096,2048]{1,0:T(8,128)(2,1)} %all-gather.9.cloned.1.call-done, bf16[8,55,4096]{2,1,0:T(8,128)(2,1)} %copy-done.1, f32[4096]{0:T(1024)S(1)} %bitcast.105, f32[4096]{0:T(1024)S(1)} %bitcast.106, f32[8,55]{1,0:T(8,128)S(1)} %add_rsqrt_fusion, ...), kind=kOutput, calls=%fused_computation.42 | convolution fusion | flops 14784675840 | bytes 40799680 | tf_op jit(solution)/shard_map/fpk,kc->fpc/dot_general | solution.py:30
  565.4 81.5 %reduce-scatter.2.cloned.1.call-done = bf16[8,55,512]{2,1,0:T(8,128)(2,1)} async-done(((bf16[8,55,4096]{2,1,0:T(8,128)(2,1)}), bf16[8,55,512]{2,1,0:T(8,128)(2,1)}) %reduce-scatter.2.cloned.1.call-update) | async-done | bytes 450576 | tf_op jit(solution)/shard_map/reduce_scatter | solution.py:70
  646.9 1.3 add_convert_fusion
  648.2 0.9 copy.32
  (51 shorter events, 5.9 us)
Async XLA Ops:
  6.5 91.0 %all-gather.5.cloned.1.call-start = ((), (), s32[]{:S(2)}) async-start(), calls=%async_computation.5 | async-start | bytes 15728640 | tf_op jit(solution)/shard_map/all_gather | solution.py:22
  9.7 3.6 copy-start.2
  12.6 153.1 %all-gather.7.cloned.1.call-start = ((), (), s32[]{:S(2)}) async-start(), calls=%async_computation.6 | async-start | bytes 5242880 | tf_op jit(solution)/shard_map/all_gather | solution.py:28
  13.3 5.9 copy-start
  116.9 16.7 %all-to-all-start = ((bf16[4,8,55,128]{3,1,2,0:T(8,128)(2,1)}), bf16[4,8,55,128]{3,1,2,0:T(8,128)(2,1)S(1)}, u32[]{:S(2)}, u32[]{:S(2)}) async-start(bf16[4,8,55,128]{3,1,2,0:T(8,128)(2,1)} %copy.24), calls=%async_computation | async-start | bytes 901120 | tf_op jit(solution)/shard_map/all_to_all | solution.py:87
  133.6 11.5 %all-to-all-start.1 = ((bf16[4,8,55,128]{3,1,2,0:T(8,128)(2,1)}), bf16[4,8,55,128]{3,1,2,0:T(8,128)(2,1)S(1)}, u32[]{:S(2)}, u32[]{:S(2)}) async-start(bf16[4,8,55,128]{3,1,2,0:T(8,128)(2,1)} %copy.25), calls=%async_computation.1 | async-start | bytes 901120 | tf_op jit(solution)/shard_map/all_to_all | solution.py:88
  145.0 11.5 %all-to-all-start.2 = ((bf16[4,8,55,128]{3,1,2,0:T(8,128)(2,1)}), bf16[4,8,55,128]{3,1,2,0:T(8,128)(2,1)S(1)}, u32[]{:S(2)}, u32[]{:S(2)}) async-start(bf16[4,8,55,128]{3,1,2,0:T(8,128)(2,1)} %copy.26), calls=%async_computation.2 | async-start | bytes 901120 | tf_op jit(solution)/shard_map/all_to_all | solution.py:89
  162.1 11.5 %all-to-all-start.3 = ((bf16[1,8,220,128]{3,1,0,2:T(8,128)(2,1)}), bf16[1,8,220,128]{3,1,0,2:T(8,128)(2,1)S(1)}, u32[]{:S(2)}, u32[]{:S(2)}) async-start(bf16[1,8,220,128]{3,1,0,2:T(8,128)(2,1)} %bitcast.90), calls=%async_computation.3 | async-start | bytes 901120 | tf_op jit(solution)/shard_map/all_to_all | solution.py:92
  165.6 156.8 %all-reduce.2.cloned.1.call-start = ((), (), s32[]{:S(2)}) async-start(), calls=%async_computation.7 | async-start | bytes 7340032 | tf_op jit(solution)/shard_map/psum | solution.py:59
  179.3 249.2 %all-gather.11.cloned.1.call-start = ((), (), s32[]{:S(2)}) async-start(), calls=%async_computation.9 | async-start | bytes 20971520 | tf_op jit(solution)/shard_map/all_gather | solution.py:28
  179.9 356.0 %all-gather.9.cloned.1.call-start = ((), (), s32[]{:S(2)}) async-start(), calls=%async_computation.8 | async-start | bytes 20971520 | tf_op jit(solution)/shard_map/all_gather | solution.py:22
  180.5 466.4 %reduce-scatter.2.cloned.1.call-start = ((), (), s32[]{:S(2)}) async-start(), calls=%async_computation.10 | async-start | bytes 4128768 | tf_op jit(solution)/shard_map/reduce_scatter | solution.py:70
  330.7 2.0 copy-start.1
Sparse Core Ops, SparseCore 0:
  12.7 84.7 all-gather.4
  99.1 39.4 all-gather.6
  179.4 142.8 all-reduce.1
  323.8 104.7 all-gather.10
  429.9 105.8 all-gather.8
  565.5 81.3 reduce-scatter.1
where the time goes:
time: 656 us
  waiting for transfers between devices  536 us (82%)
  matrix products  57.3 us (9%)
  other arithmetic  21.1 us (3%)
  starting transfers between devices  14.3 us (2%)
  between operations  13.6 us (2%)
  local copies, waits for them, and re-layouts  13 us (2%)
    all_gather x2, waiting for transfers between devices, project_rows(): lax.all_gather(weight, 'sp', axis=0, tiled=True)  182 us
    psum x1, waiting for transfers between devices, attention_combine(): lax.psum(partial_value.astype(jnp.bfloat16), 'tp').astype(jnp.float32)  142 us
    all_gather x2, waiting for transfers between devices, project_cols(): portion = lax.all_gather(weight, 'sp', axis=1, tiled=True)  94.7 us
    reduce_scatter x1, waiting for transfers between devices, mlp_combine(): lax.psum_scatter(partial_value.astype(jnp.bfloat16), 'tp', scatter_dimens...  81.5 us
    dot_general x2, matrix products, project_cols(): jnp.einsum(einsum_form, operand, shaped, preferred_element_type=jnp.float32)  35.2 us
    dot_general x1, matrix products, project_rows(): jnp.einsum(einsum_form, operand, lax.all_gather(weight, 'sp', axis=0, til...  18.3 us
    reduce_sum x2, other arithmetic, normalize(): center = jnp.mean(values, axis=-1, keepdims=True)  14.1 us
  transfers between devices with their start and end apart: 10, of which 9 were waited for; matrix products, arithmetic and copies ran while one was open for 7% of the time, Pallas kernels for 0%

commit v1 on v0

--- a/solution.py
+++ b/solution.py
@@ -56,7 +56,9 @@
 
 
 def attention_combine(base, partial_value, gate):
-    summed = lax.psum(partial_value.astype(jnp.bfloat16), "tp").astype(jnp.float32)
+    summed = jnp.sum(lax.all_gather(partial_value.astype(jnp.bfloat16), "tp"), axis=0).astype(
+        jnp.float32
+    )
     full = (base.astype(jnp.float32) + gate * summed).astype(jnp.bfloat16)
     return full
 

time: 656 us -> 1070 us (1.63)
  waiting for transfers between devices: 536 us -> 923 us
  other arithmetic: 21.1 us -> 42 us
    all_gather x0 -> x1, waiting for transfers between devices: none -> 548 us  [attention_combine(): lax.all_gather(partial_value.astype(jnp.bfloat16), 'tp')]
    psum x1 -> x0, waiting for transfers between devices: 142 us -> none  [attention_combine(): lax.psum(partial_value.astype(jnp.bfloat16), 'tp').astype(jnp.float32)]
    all_gather x2, waiting for transfers between devices: 182 us -> 149 us  [project_rows(): lax.all_gather(weight, 'sp', axis=0, tiled=True)]
    reduce_sum x0 -> x1, other arithmetic: none -> 14.2 us  [attention_combine(): jnp.sum(lax.all_gather(partial_value.astype(jnp.bfloat16), 'tp'), axis=0)]
    all_gather x2, waiting for transfers between devices: 94.7 us -> 107 us  [project_cols(): portion = lax.all_gather(weight, 'sp', axis=1, tiled=True)]
  transfers between devices with their start and end apart: 10 -> 10, of which waited for: 9 -> 9; matrix products, arithmetic and copies ran while one was open for 7% -> 6% of each run, Pallas kernels for 0% -> 0%
where the time goes in v1:
time: 1070 us
  waiting for transfers between devices  923 us (86%)
  matrix products  56.9 us (5%)
  other arithmetic  42 us (4%)
  local copies, waits for them, and re-layouts  16.6 us (2%)
  starting transfers between devices  14.2 us (1%)
  between operations  13.9 us (1%)
    all_gather x1, waiting for transfers between devices, attention_combine(): lax.all_gather(partial_value.astype(jnp.bfloat16), 'tp')  548 us
    all_gather x2, waiting for transfers between devices, project_rows(): lax.all_gather(weight, 'sp', axis=0, tiled=True)  149 us
    all_gather x2, waiting for transfers between devices, project_cols(): portion = lax.all_gather(weight, 'sp', axis=1, tiled=True)  107 us
    reduce_scatter x1, waiting for transfers between devices, mlp_combine(): lax.psum_scatter(partial_value.astype(jnp.bfloat16), 'tp', scatter_dimens...  81.5 us
    dot_general x2, matrix products, project_cols(): jnp.einsum(einsum_form, operand, shaped, preferred_element_type=jnp.float32)  34.3 us
  transfers between devices with their start and end apart: 10, of which 9 were waited for; matrix products, arithmetic and copies ran while one was open for 6% of the time, Pallas kernels for 0%

profile of v1, /device:TPU:0, one launch (start us, length us, event | category | flops | bytes accessed | tf_op | source)
XLA Modules:
  0.0 1067.0 jit_solution(6587318291457277410)
XLA Ops:
  6.5 3.2 copy.35
  9.7 2.8 copy.36
  13.4 5.8 convert_reduce_fusion
  19.2 3.9 fusion.23
  23.1 74.4 %all-gather.7.cloned.1.call-done = bf16[4096,3,4,128]{3,0,2,1:T(8,128)(2,1)} async-done(((bf16[1024,3,4,128]{3,0,2,1:T(8,128)(2,1)}), bf16[4096,3,4,128]{3,0,2,1:T(8,128)(2,1)}) %all-gather.7.cloned.1.call-update) | async-done | bytes 12582928 | tf_op jit(solution)/shard_map/all_gather | solution.py:22
  97.5 18.7 %fusion.69 = bf16[3,4,8,55,128]{4,3,1,0,2:T(8,128)(2,1)S(1)} fusion(bf16[4096,3,4,128]{3,0,2,1:T(8,128)(2,1)} %all-gather.7.cloned.1.call-done, f32[4096]{0:T(1024)S(1)} %bitcast.109, f32[4096]{0:T(1024)S(1)} %bitcast.110, f32[8,55]{1,0:T(8,128)S(1)} %add_rsqrt_fusion.1, f32[8,55]{1,0:T(8,128)S(1)} %broadcast_multiply_fusion.1, bf16[8,55,4096]{2,0,1:T(8,128)(2,1)} %param.8), kind=kOutput, calls=%fused_computation.65 | convolution fusion | flops 5547970560 | bytes 17575360 | tf_op jit(solution)/shard_map/fpd,dshe->shfpe/dot_general | solution.py:19
  116.4 0.9 copy.37
  117.3 3.5 all-to-all-start
  120.8 0.9 copy.38
  121.7 12.3 %all-to-all-done = bf16[4,8,55,128]{3,1,2,0:T(8,128)(2,1)S(1)} async-done(((bf16[4,8,55,128]{3,1,2,0:T(8,128)(2,1)}), bf16[4,8,55,128]{3,1,2,0:T(8,128)(2,1)S(1)}, u32[]{:S(2)}, u32[]{:S(2)}) %all-to-all-start) | async-done | bytes 450592 | tf_op jit(solution)/shard_map/all_to_all | solution.py:89
  134.0 3.5 all-to-all-start.1
  137.5 0.9 copy.39
  138.4 7.0 all-to-all-done.1
  145.5 3.5 all-to-all-start.2
  149.1 7.8 all-to-all-done.2
  157.0 4.6 while.10
  161.6 0.9 copy.69
  162.5 3.5 all-to-all-start.3
  166.1 7.9 all-to-all-done.3
  174.0 4.5 bitcast_convert_fusion
  178.5 3.8 copy.45
  183.7 548.0 %all-gather.15.cloned.1.call-done = bf16[64,55,4096]{2,0,1:T(8,128)(2,1)} async-done(((bf16[8,55,4096]{2,0,1:T(8,128)(2,1)}), bf16[64,55,4096]{2,0,1:T(8,128)(2,1)}) %all-gather.15.cloned.1.call-update) | async-done | bytes 28835856 | tf_op jit(solution)/shard_map/all_gather | solution.py:59
  731.7 14.2 %bitcast_reduce_fusion = bf16[8,55,4096]{2,0,1:T(8,128)(2,1)} fusion(bf16[64,55,4096]{2,0,1:T(8,128)(2,1)} %all-gather.15.cloned.1.call-done), kind=kLoop, calls=%fused_computation.17 | loop fusion | flops 12615680 | bytes 32440320 | tf_op jit(solution)/shard_map/reduce_sum | solution.py:59
  745.9 15.1 %convert_reduce_fusion.1 = (f32[8,55]{1,0:T(8,128)S(1)}, bf16[8,55,4096]{2,1,0:T(8,128)(2,1)S(1)}) fusion(bf16[8,55,4096]{2,0,1:T(8,128)(2,1)} %bitcast_reduce_fusion, f32[4096]{0:T(1024)S(1)} %bitcast.106, bf16[8,55,4096]{2,0,1:T(8,128)(2,1)} %param.8), kind=kLoop, calls=%fused_computation.28 | loop fusion | flops 12615240 | bytes 10831584 | tf_op jit(solution)/shard_map/reduce_sum | solution.py:12
  761.0 1.8 copy-done.1
  762.8 1.1 fusion.27
  763.9 75.1 %all-gather.11.cloned.1.call-done = bf16[4096,2048]{1,0:T(8,128)(2,1)} async-done(((bf16[1024,2048]{1,0:T(8,128)(2,1)}), bf16[4096,2048]{1,0:T(8,128)(2,1)}) %all-gather.11.cloned.1.call-update) | async-done | bytes 16777232 | tf_op jit(solution)/shard_map/all_gather | solution.py:22
  839.0 107.3 %all-gather.13.cloned.1.call-done = bf16[2048,4096]{1,0:T(8,128)(2,1)} async-done(((bf16[2048,1024]{1,0:T(8,128)(2,1)}), bf16[2048,4096]{1,0:T(8,128)(2,1)}) %all-gather.13.cloned.1.call-update) | async-done | bytes 16777232 | tf_op jit(solution)/shard_map/all_gather | solution.py:28
  946.3 29.8 %fusion.32 = bf16[8,55,4096]{2,1,0:T(8,128)(2,1)} fusion(bf16[2048,4096]{1,0:T(8,128)(2,1)} %all-gather.13.cloned.1.call-done, bf16[4096,2048]{1,0:T(8,128)(2,1)} %all-gather.11.cloned.1.call-done, bf16[8,55,4096]{2,1,0:T(8,128)(2,1)} %copy-done.1, f32[4096]{0:T(1024)S(1)} %bitcast.107, f32[4096]{0:T(1024)S(1)} %bitcast.108, ...), kind=kOutput, calls=%fused_computation.43 | convolution fusion | flops 14784675840 | bytes 40799680 | tf_op jit(solution)/shard_map/fpk,kc->fpc/dot_general | solution.py:30
  976.2 81.5 %reduce-scatter.2.cloned.1.call-done = bf16[8,55,512]{2,1,0:T(8,128)(2,1)} async-done(((bf16[8,55,4096]{2,1,0:T(8,128)(2,1)}), bf16[8,55,512]{2,1,0:T(8,128)(2,1)}) %reduce-scatter.2.cloned.1.call-update) | async-done | bytes 450576 | tf_op jit(solution)/shard_map/reduce_scatter | solution.py:72
  1057.7 1.3 add_convert_fusion
  1059.0 0.9 copy.47
  (53 shorter events, 7.1 us)
Async XLA Ops:
  6.5 91.0 %all-gather.7.cloned.1.call-start = ((), (), s32[]{:S(2)}) async-start(), calls=%async_computation.5 | async-start | bytes 15728640 | tf_op jit(solution)/shard_map/all_gather | solution.py:22
  9.7 3.6 copy-start.2
  12.6 153.5 %all-gather.9.cloned.1.call-start = ((), (), s32[]{:S(2)}) async-start(), calls=%async_computation.6 | async-start | bytes 5242880 | tf_op jit(solution)/shard_map/all_gather | solution.py:28
  13.3 5.9 copy-start
  117.3 16.7 %all-to-all-start = ((bf16[4,8,55,128]{3,1,2,0:T(8,128)(2,1)}), bf16[4,8,55,128]{3,1,2,0:T(8,128)(2,1)S(1)}, u32[]{:S(2)}, u32[]{:S(2)}) async-start(bf16[4,8,55,128]{3,1,2,0:T(8,128)(2,1)} %copy.37), calls=%async_computation | async-start | bytes 901120 | tf_op jit(solution)/shard_map/all_to_all | solution.py:89
  134.0 11.5 %all-to-all-start.1 = ((bf16[4,8,55,128]{3,1,2,0:T(8,128)(2,1)}), bf16[4,8,55,128]{3,1,2,0:T(8,128)(2,1)S(1)}, u32[]{:S(2)}, u32[]{:S(2)}) async-start(bf16[4,8,55,128]{3,1,2,0:T(8,128)(2,1)} %copy.38), calls=%async_computation.1 | async-start | bytes 901120 | tf_op jit(solution)/shard_map/all_to_all | solution.py:90
  145.5 11.5 %all-to-all-start.2 = ((bf16[4,8,55,128]{3,1,2,0:T(8,128)(2,1)}), bf16[4,8,55,128]{3,1,2,0:T(8,128)(2,1)S(1)}, u32[]{:S(2)}, u32[]{:S(2)}) async-start(bf16[4,8,55,128]{3,1,2,0:T(8,128)(2,1)} %copy.39), calls=%async_computation.2 | async-start | bytes 901120 | tf_op jit(solution)/shard_map/all_to_all | solution.py:91
  162.5 11.5 %all-to-all-start.3 = ((bf16[1,8,220,128]{3,1,0,2:T(8,128)(2,1)}), bf16[1,8,220,128]{3,1,0,2:T(8,128)(2,1)S(1)}, u32[]{:S(2)}, u32[]{:S(2)}) async-start(bf16[1,8,220,128]{3,1,0,2:T(8,128)(2,1)} %bitcast.92), calls=%async_computation.3 | async-start | bytes 901120 | tf_op jit(solution)/shard_map/all_to_all | solution.py:94
  166.0 565.7 %all-gather.15.cloned.1.call-start = ((), (), s32[]{:S(2)}) async-start(), calls=%async_computation.10 | async-start | bytes 32440320 | tf_op jit(solution)/shard_map/all_gather | solution.py:59
  182.4 656.7 %all-gather.11.cloned.1.call-start = ((), (), s32[]{:S(2)}) async-start(), calls=%async_computation.7 | async-start | bytes 20971520 | tf_op jit(solution)/shard_map/all_gather | solution.py:22
  182.9 763.4 %all-gather.13.cloned.1.call-start = ((), (), s32[]{:S(2)}) async-start(), calls=%async_computation.8 | async-start | bytes 20971520 | tf_op jit(solution)/shard_map/all_gather | solution.py:28
  183.5 874.2 %reduce-scatter.2.cloned.1.call-start = ((), (), s32[]{:S(2)}) async-start(), calls=%async_computation.9 | async-start | bytes 4128768 | tf_op jit(solution)/shard_map/reduce_scatter | solution.py:72
  761.0 1.8 copy-start.1
Sparse Core Ops, SparseCore 0:
  12.7 84.7 all-gather.6
  99.1 39.2 all-gather.8
  182.5 549.1 all-gather.14
  733.1 105.8 all-gather.10
  840.4 105.8 all-gather.12
  976.3 81.3 reduce-scatter.1
